TPU v7x, 32 devices: a whole 2x2x4 slice. The times are simulated.
32 devices in a mesh: nodes: 32 (over z, y, x, core).
Axes of the slice: x: 2, y: 2, z: 4, core: 2. Of those that a mesh axis runs over, the one named last changes fastest.
Arguments:
- features: bfloat16 [524288, 128], P('nodes'), may hold values from -6 to 6
- nbr_owner: int32 [1024, 32], P('nodes'), may hold values from 0 to 31, all different within a row; in each aligned block of 32 rows (0 to 31, 32 to 63, ...) at most 32 rows name the same one
- nbr_local: int32 [1024, 32], P('nodes'), may hold values from 0 to 16383
- ppr_weight: float32 [1024, 32], P('nodes'), may hold values from 0.01 to 0.1
- labels: int32 [1024], P('nodes'), may hold values from 0 to 171
- w_first: bfloat16 [128, 512], replicated, may hold values from -0.5 to 0.5
- w_second: bfloat16 [512, 512], replicated, may hold values from -0.25 to 0.25
- w_third: bfloat16 [512, 172], replicated, may hold values from -0.25 to 0.25
Outputs:
- loss: float32 [], replicated
- seed_logits: float32 [1024, 172], P('nodes')
- grad_first: float32 [128, 512], replicated
- grad_second: float32 [512, 512], replicated
- grad_third: float32 [512, 172], replicated
Inputs may be any that keep to these rules, and one draw needn't show every extreme that they name: `nbr_owner`: each row names 32 different devices; among the rows of one device no device is named by more than 32 rows.
All inputs are finite; a program needn't handle non-finite values.
Results may differ from a plain program's by a relative error of at most 0.01.
The roundings to bfloat16 on the way count: a program that leaves them out, or rounds other values in their place, can miss the bound.
Values may be sent and summed in bfloat16 or wider, within the bound.
A program may use at most 64 MiB of HBM per device.

v0:
```python
import jax
import jax.numpy as jnp
from jax import lax
from jax.sharding import PartitionSpec as P


def forward_rows(row_block, w_first, w_second, w_third):
    first_pre = jnp.dot(row_block, w_first, preferred_element_type=jnp.float32)
    first_act = jnp.maximum(first_pre, 0.0).astype(jnp.bfloat16)
    second_pre = jnp.dot(first_act, w_second, preferred_element_type=jnp.float32)
    second_act = jnp.maximum(second_pre, 0.0).astype(jnp.bfloat16)
    row_logits = jnp.dot(second_act, w_third, preferred_element_type=jnp.float32)
    return ((first_pre > 0, first_act, second_pre > 0, second_act), row_logits)


def backward_rows(row_block, cached, logit_grads, w_second, w_third):
    first_mask, first_act, second_mask, second_act = cached
    grad_third = jnp.dot(second_act.T, logit_grads, preferred_element_type=jnp.float32)
    second_grad = jnp.where(
        second_mask, jnp.dot(logit_grads, w_third.T, preferred_element_type=jnp.float32), 0.0
    ).astype(jnp.bfloat16)
    grad_second = jnp.dot(first_act.T, second_grad, preferred_element_type=jnp.float32)
    first_grad = jnp.where(
        first_mask, jnp.dot(second_grad, w_second.T, preferred_element_type=jnp.float32), 0.0
    ).astype(jnp.bfloat16)
    grad_first = jnp.dot(row_block.T, first_grad, preferred_element_type=jnp.float32)
    return (grad_first, grad_second, grad_third)


def seed_loss(seed_logits, labels, total_seeds):
    classes = seed_logits.shape[1]
    highest = jnp.max(seed_logits, axis=1, keepdims=True)
    log_total = jnp.log(jnp.sum(jnp.exp(seed_logits - highest), axis=1, keepdims=True)) + highest
    onehot = (labels[:, None] == jnp.arange(classes, dtype=jnp.int32)[None, :]).astype(jnp.float32)
    loss_terms = jnp.sum(log_total[:, 0] - jnp.sum(onehot * seed_logits, axis=1))
    logit_grad = (jnp.exp(seed_logits - log_total) - onehot) / total_seeds
    return (loss_terms, logit_grad)


def on_device(features, nbr_owner, nbr_local, ppr_weight, labels, w_first, w_second, w_third):
    groups = lax.axis_size("nodes")
    seed_count, neighbours = nbr_owner.shape
    capacity = min(seed_count, 2 * seed_count * neighbours // groups)
    classes = w_third.shape[1]
    total_seeds = float(seed_count * groups)
    owner_table = jnp.arange(groups, dtype=jnp.int32)
    per_seed = jnp.sum(
        (nbr_owner[:, :, None] == owner_table[None, None, :]).astype(jnp.int32), axis=1
    )
    earlier = jnp.cumsum(per_seed, axis=0) - per_seed
    position = jnp.take_along_axis(earlier, nbr_owner, axis=1)
    slot_index = (nbr_owner * capacity + position).reshape(-1)
    outgoing = jnp.zeros((groups * capacity,), jnp.int32).at[slot_index].set(nbr_local.reshape(-1))
    requested = lax.all_to_all(
        outgoing.reshape(groups, capacity), "nodes", split_axis=0, concat_axis=0, tiled=True
    )
    local_rows = jnp.take(features, requested.reshape(-1), axis=0)
    arrived = lax.all_to_all(
        local_rows.reshape(groups, capacity, local_rows.shape[1]),
        "nodes",
        split_axis=0,
        concat_axis=0,
        tiled=True,
    )
    row_block = jnp.take(
        arrived.reshape(groups * capacity, local_rows.shape[1]), slot_index, axis=0
    )
    cached, row_logits = forward_rows(row_block, w_first, w_second, w_third)
    seed_logits = jnp.sum(
        ppr_weight[:, :, None] * row_logits.reshape(seed_count, neighbours, classes), axis=1
    )
    loss_terms, logit_grad = seed_loss(seed_logits, labels, total_seeds)
    weighted = (
        (ppr_weight[:, :, None] * logit_grad[:, None, :]).astype(jnp.bfloat16).reshape(-1, classes)
    )
    gradients = backward_rows(row_block, cached, weighted, w_second, w_third)
    loss_sum, grad_first, grad_second, grad_third = lax.psum(
        (loss_terms, gradients[0], gradients[1], gradients[2]), "nodes"
    )
    return (loss_sum / total_seeds, seed_logits, grad_first, grad_second, grad_third)


def solution(mesh):
    return jax.shard_map(
        on_device,
        mesh=mesh,
        in_specs=(
            P("nodes", None),
            P("nodes", None),
            P("nodes", None),
            P("nodes", None),
            P("nodes"),
            P(),
            P(),
            P(),
        ),
        out_specs=(P(), P("nodes", None), P(), P(), P()),
        check_vma=False,
    )
```

profile of v0, /device:TPU:9, one launch (start us, length us, event | category | flops | bytes accessed | tf_op | source)
XLA Modules:
  0.0 214.9 jit_solution(12515252225469769063)
XLA Ops:
  7.2 1.0 convert_reduce_fusion
  8.2 0.7 bitcast_or_fusion
  8.9 0.8 reshape.201
  9.8 7.1 %gather_fusion.2 = s32[1024]{0:T(1024)S(1)} fusion(s32[32,32]{1,0:T(8,128)S(1)} %sub.33, s32[1024]{0:T(1024)S(1)} %reshape.191), kind=kCustom, calls=%fused_computation.2 | custom fusion | bytes 16384 | tf_op jit(solution)/shard_map/jit(take_along_axis)/gather | solution.py:51
  17.1 4.3 %scatter_custom_fusion = s32[1024]{0:T(1024)S(1)} fusion(s32[1024]{0:T(1024)S(1)} %bitcast.28, s32[1024]{0:T(1024)S(1)} %reshape.201, s32[]{:T(128)} %constant.37.clone.1), kind=kCustom, calls=%fused_computation.37 | custom fusion | bytes 4100 | tf_op jit(solution)/shard_map/scatter | solution.py:53
  21.4 0.1 all_to_all.9
  21.5 11.7 %all_to_all.14 = s32[32,1,32]{2,1,0:T(1,128)S(1)} all-to-all(s32[32,1,32]{2,1,0:T(1,128)S(1)} %all_to_all.9), channel_id=1, replica_groups=mesh['nodes'=32] {'nodes'}, dimensions={0} | all-to-all | bytes 8192 | tf_op jit(solution)/shard_map/all_to_all | solution.py:54
  33.3 0.5 broadcast.139
  33.8 0.7 reduce.3
  34.6 5.6 %gather_fusion = bf16[1024,128]{1,0:T(8,128)(2,1)S(1)} fusion(bf16[16384,128]{1,0:T(8,128)(2,1)} %param.8, s32[1024]{0:T(1024)S(1)} %broadcast_clamp_fusion.1), kind=kCustom, calls=%fused_computation | custom fusion | bytes 528384 | tf_op jit(solution)/shard_map/jit(_take)/gather | solution.py:57
  40.2 0.9 broadcast_select_fusion.1
  41.1 4.1 %all-to-all-start.1 = ((bf16[32,32,128]{2,1,0:T(8,128)(2,1)}), bf16[32,32,128]{2,1,0:T(8,128)(2,1)S(1)}, u32[]{:S(2)}, u32[]{:S(2)}) async-start(bf16[32,32,128]{2,1,0:T(8,128)(2,1)} %broadcast_select_fusion.1), calls=%async_computation.1 | async-start | bytes 524288 | tf_op jit(solution)/shard_map/all_to_all | solution.py:58
  45.4 8.6 %all-to-all-done.1 = bf16[32,32,128]{2,1,0:T(8,128)(2,1)S(1)} async-done(((bf16[32,32,128]{2,1,0:T(8,128)(2,1)}), bf16[32,32,128]{2,1,0:T(8,128)(2,1)S(1)}, u32[]{:S(2)}, u32[]{:S(2)}) %all-to-all-start.1) | async-done | bytes 262176 | tf_op jit(solution)/shard_map/all_to_all | solution.py:58
  54.0 3.2 %gather_fusion.1 = bf16[1024,128]{1,0:T(8,128)(2,1)S(1)} fusion(bf16[1024,128]{1,0:T(8,128)(2,1)S(1)} %bitcast.25, s32[1024]{0:T(1024)S(1)} %broadcast_clamp_fusion), kind=kCustom, calls=%fused_computation.1 | custom fusion | bytes 528384 | tf_op jit(solution)/shard_map/jit(_take)/gather | solution.py:65
  57.2 0.5 fusion.7
  57.7 0.7 fusion.4
  58.4 0.6 copy-done.1
  59.0 0.5 multiply_reduce_fusion
  59.5 0.1 reduce_max.9
  59.7 0.2 select_reduce_fusion
  59.9 0.6 subtract_reduce_fusion
  60.5 0.1 subtract_multiply_fusion
  60.6 0.2 fusion.1
  60.8 1.1 fusion.5
  61.9 1.4 select_convert_fusion.1
  63.3 3.7 %fusion = f32[128,512]{1,0:T(8,128)} fusion(f32[1024,512]{1,0:T(8,128)} %copy-done.1, bf16[1024,512]{1,0:T(8,128)(2,1)} %select_convert_fusion.1, bf16[512,512]{1,0:T(8,128)(2,1)S(1)} %copy-done, bf16[1024,128]{1,0:T(8,128)(2,1)S(1)} %gather_fusion.1, pred[1024]{0:T(1024)(128)(4,1)S(1)} %compare_and_fusion.1), kind=kOutput, calls=%fused_computation.8 | convolution fusion | flops 672792576 | bytes 4195328 | tf_op jit(solution)/shard_map/dot_general | solution.py:26
  67.0 3.0 %fusion.3 = f32[512,512]{1,0:T(8,128)} fusion(bf16[1024,512]{1,0:T(8,128)(2,1)} %select_convert_fusion.1, f32[1024,512]{1,0:T(8,128)S(1)} %copy-done.2), kind=kOutput, calls=%fused_computation.15 | convolution fusion | flops 537919488 | bytes 4194304 | tf_op jit(solution)/shard_map/dot_general | solution.py:22
  70.1 39.7 %psum.28 = f32[]{:T(128)} all-reduce(f32[]{:T(128)} %get-tuple-element.10), channel_id=1, replica_groups=mesh['nodes'=32] {'nodes'}, use_global_device_ids=true, to_apply=%region_8.9 | all-reduce | flops 1 | bytes 8 | tf_op jit(solution)/shard_map/psum | solution.py:77
  110.4 91.7 %all-reduce.3.cloned.1.call-done = (f32[128,512]{1,0:T(8,128)}, f32[512,512]{1,0:T(8,128)}, f32[512,172]{0,1:T(8,128)}) async-done(((f32[128,512]{1,0:T(8,128)}, f32[512,512]{1,0:T(8,128)}, f32[512,172]{0,1:T(8,128)}), (f32[128,512]{1,0:T(8,128)}, f32[512,512]{1,0:T(8,128)}, f32[512,172]{0,1:T(8,128)})) %all-reduce.3.cloned.1.call-update) | async-done | bytes 1662992 | tf_op jit(solution)/shard_map/psum | solution.py:77
  202.2 1.7 copy.20
  203.9 2.3 %copy.21 = f32[512,512]{1,0:T(8,128)} copy(f32[512,512]{1,0:T(8,128)} %get-tuple-element.15) | data formatting | bytes 2097152
  206.1 0.7 copy.22
  (36 shorter events, 0.7 us)
Async XLA Ops:
  7.2 50.5 %copy-start = (bf16[512,512]{1,0:T(8,128)(2,1)S(1)}, bf16[512,512]{1,0:T(8,128)(2,1)}, u32[]{:S(2)}) copy-start(bf16[512,512]{1,0:T(8,128)(2,1)} %param.14) | copy-start | bytes 1572868
  9.8 7.2 %copy-start.6 = (s32[32,32]{1,0:T(8,128)S(1)}, s32[32,32]{1,0:T(8,128)}, u32[]{:S(2)}) copy-start(s32[32,32]{1,0:T(8,128)} %param.9) | copy-start | bytes 12292
  16.9 28.4 %copy-start.8 = (f32[32,32]{1,0:T(8,128)S(1)}, f32[32,32]{1,0:T(8,128)}, u32[]{:S(2)}) copy-start(f32[32,32]{1,0:T(8,128)} %param.11) | copy-start | bytes 12292
  40.2 17.0 %copy-start.7 = (bf16[128,512]{1,0:T(8,128)(2,1)S(1)}, bf16[128,512]{1,0:T(8,128)(2,1)}, u32[]{:S(2)}) copy-start(bf16[128,512]{1,0:T(8,128)(2,1)} %param.13) | copy-start | bytes 393220
  41.1 12.9 %all-to-all-start.1 = ((bf16[32,32,128]{2,1,0:T(8,128)(2,1)}), bf16[32,32,128]{2,1,0:T(8,128)(2,1)S(1)}, u32[]{:S(2)}, u32[]{:S(2)}) async-start(bf16[32,32,128]{2,1,0:T(8,128)(2,1)} %broadcast_select_fusion.1), calls=%async_computation.1 | async-start | bytes 524288 | tf_op jit(solution)/shard_map/all_to_all | solution.py:58
  45.2 157.0 %all-reduce.3.cloned.1.call-start = ((), (), s32[]{:S(2)}) async-start(), calls=%async_computation.2 | async-start | bytes 3342336 | tf_op jit(solution)/shard_map/psum | solution.py:77
  57.7 1.4 copy-start.1
  57.7 1.3 copy-start.3
  59.0 0.7 copy-start.9
  59.5 3.8 %copy-start.4 = (f32[32,172]{1,0:T(8,128)}, f32[32,172]{1,0:T(8,128)S(1)}, u32[]{:S(2)}) copy-start(f32[32,172]{1,0:T(8,128)S(1)} %multiply_reduce_fusion) | copy-start | bytes 66052
  63.3 3.7 %copy-start.2 = (f32[1024,512]{1,0:T(8,128)S(1)}, f32[1024,512]{1,0:T(8,128)}, u32[]{:S(2)}) copy-start(f32[1024,512]{1,0:T(8,128)} %copy-done.1) | copy-start | bytes 6291460
  202.2 4.0 %copy-start.5 = (f32[512,172]{0,1:T(8,128)S(1)}, f32[512,172]{0,1:T(8,128)}, u32[]{:S(2)}) copy-start(f32[512,172]{0,1:T(8,128)} %get-tuple-element.16) | copy-start | bytes 1056772
Sparse Core Ops, SparseCore 0:
  70.2 131.9 all-reduce.2
where the time goes:
time: 219 us; the launch traced here: 215 us
  waiting for transfers between devices  100 us (46%)
  blocking collectives  51.4 us (23%)
  local copies, waits for them, and re-layouts  27.5 us (13%)
  between operations  16 us (7%)
  matrix products  10.9 us (5%)
  other arithmetic  4.63 us (2%)
  starting transfers between devices  4.12 us (2%)
    psum x1, waiting for transfers between devices, on_device(): lax.psum((loss_terms, gradients[0], gradients[1], gradients[2]), 'nodes')  91.7 us
    psum x1, blocking collectives, on_device(): lax.psum((loss_terms, gradients[0], gradients[1], gradients[2]), 'nodes')  39.7 us
    all_to_all x1, blocking collectives, on_device(): lax.all_to_all(outgoing.reshape(groups, capacity), 'nodes', split_axis=0,...  11.7 us
    all_to_all x1, waiting for transfers between devices, on_device(): lax.all_to_all(local_rows.reshape(groups, capacity, local_rows.shape[1]),...  8.57 us
    gather x3, local copies, waits for them, and re-layouts, on_device(): position = jnp.take_along_axis(earlier, nbr_owner, axis=1)  7.2 us
    gather x1, local copies, waits for them, and re-layouts, on_device(): local_rows = jnp.take(features, requested.reshape(-1), axis=0)  5.61 us
    unnamed x23, local copies, waits for them, and re-layouts  5.45 us
  transfers between devices with their start and end apart: 2, of which 2 were waited for; matrix products, arithmetic and copies ran while one was open for 0% of the time, Pallas kernels for 0%

commit v1 on v0

v1 whole, which is shorter than its diff:
```python
import functools

import jax
import jax.numpy as jnp
from jax import lax
from jax.experimental import pallas as pl
from jax.experimental.pallas import tpu as pltpu
from jax.sharding import PartitionSpec as P

MESH = pl.DeviceIdType.MESH
F32 = jnp.float32
BF16 = jnp.bfloat16
LANES = 128


def tdot(a, b):
    return lax.dot_general(a, b, (((0,), (0,)), ((), ())), preferred_element_type=F32)


def dott(a, b):
    return lax.dot_general(a, b, (((1,), (1,)), ((), ())), preferred_element_type=F32)


def kernel(
    dims,
    idx_out, owner, ppr, labels, feats, w1, w2, w3,
    loss_ref, logits_ref, g1_ref, g2_ref, g3_ref,
    feat16, feat32, idx_in, idx_smem, stage, row_send, rows, wbuf, w3p, h1b, h2b,
    zacc, gbuf, loss_in, acc, pair_send, pair_recv, part_send, part_recv, full,
    feat_sem, smem_sem, idx_ss, idx_rs, row_ss, row_rs, loss_ss, loss_rs,
    pair_ss, pair_rs, part_ss, part_rs, full_ss, full_rs, relay_ss, relay_rs,
):
    groups, seeds, classes, per, pieces = dims
    chips = groups // 2
    me = lax.axis_index("nodes")
    chip = me // 2
    core = me % 2
    partner = chip * 2 + (1 - core)
    nodes, feat_dim = feats.shape
    hidden = w1.shape[1]
    padded = w3p.shape[1]
    piece = nodes // pieces

    def remote(src, dst, ss, rs, dev):
        return pltpu.make_async_remote_copy(
            src_ref=src, dst_ref=dst, send_sem=ss, recv_sem=rs, device_id=(dev,), device_id_type=MESH
        )

    def feat_copy(i):
        at = pl.ds(i * piece, piece)
        return pltpu.make_async_copy(feats.at[at], feat16.at[at], feat_sem.at[i])

    for i in range(pieces):
        feat_copy(i).start()

    def others(body, size=groups, mine=me):
        def step(d, carry):
            body(lax.rem(mine + d, size))
            return carry
        lax.fori_loop(1, size, step, 0)

    barrier = pltpu.get_barrier_semaphore()
    others(lambda p: pl.semaphore_signal(barrier, inc=1, device_id=(p,), device_id_type=MESH))
    pl.semaphore_wait(barrier, groups - 1)

    def idx_copy(p, slot):
        return remote(idx_out.at[p], idx_in.at[slot], idx_ss.at[p], idx_rs.at[slot], p)

    others(lambda p: idx_copy(p, me).start())
    idx_in[me] = idx_out[me]

    w3p[...] = jnp.zeros_like(w3p)
    w3p[:, :classes] = w3[...]

    own = owner[...]
    score = ppr[...]

    def weight_step(o, carry):
        w = jnp.sum(jnp.where(own == o, score, 0.0), axis=1, keepdims=True)
        wbuf[pl.ds(pl.multiple_of(o * seeds, 8), seeds), :] = jnp.broadcast_to(w, (seeds, LANES))
        return carry

    lax.fori_loop(0, groups, weight_step, 0)

    block = min(512, piece)
    for i in range(pieces):
        feat_copy(i).wait()

        def widen(j, carry, i=i):
            at = pl.ds(pl.multiple_of(i * piece + j * block, 16), block)
            feat32[at, :] = feat16[at, :].astype(F32)
            return carry

        lax.fori_loop(0, piece // block, widen, 0)

    others(lambda p: idx_copy(p, p).wait_recv())
    to_smem = pltpu.make_async_copy(idx_in, idx_smem, smem_sem)
    to_smem.start()
    to_smem.wait()

    def collect(p):
        for i in range(seeds):
            stage[i : i + 1, :] = feat32[pl.ds(idx_smem[p, 0, i], 1), :]
        return stage[...].astype(BF16)

    def row_copy(p, slot):
        return remote(row_send.at[p], rows.at[slot], row_ss.at[p], row_rs.at[slot], p)

    def send_rows(p):
        row_send[p] = collect(p)
        row_copy(p, me).start()

    others(send_rows)
    rows[me] = collect(me)
    others(lambda p: idx_copy(p, me).wait_send())
    others(lambda p: row_copy(p, p).wait_recv())

    step_owners = min(groups, max(1, 512 // seeds))
    step_rows = step_owners * seeds
    steps = groups // step_owners
    zacc[...] = jnp.zeros_like(zacc)

    def wide(at):
        return jnp.concatenate([wbuf[at, :]] * (padded // LANES), axis=1)

    def forward(t, carry):
        at = pl.ds(pl.multiple_of(t * step_rows, step_rows), step_rows)
        x = rows[pl.ds(t * step_owners, step_owners)].reshape(step_rows, feat_dim)
        h1 = jnp.maximum(jnp.dot(x, w1[...], preferred_element_type=F32), 0.0).astype(BF16)
        h1b[at, :] = h1
        h2 = jnp.maximum(jnp.dot(h1, w2[...], preferred_element_type=F32), 0.0).astype(BF16)
        h2b[at, :] = h2
        z = jnp.dot(h2, w3p[...], preferred_element_type=F32) * wide(at)
        zacc[...] += jnp.sum(z.reshape(step_owners, seeds, padded), axis=0)
        return carry

    lax.fori_loop(0, steps, forward, 0)

    logits = zacc[...]
    logits_ref[...] = logits[:, :classes]
    col = lax.broadcasted_iota(jnp.int32, (seeds, padded), 1)
    valid = col < classes
    highest = jnp.max(jnp.where(valid, logits, -3.0e38), axis=1, keepdims=True)
    expd = jnp.where(valid, jnp.exp(jnp.minimum(logits - highest, 0.0)), 0.0)
    lse = jnp.log(jnp.sum(expd, axis=1, keepdims=True)) + highest
    onehot = jnp.where(col == labels[...], 1.0, 0.0)
    terms = lse - jnp.sum(onehot * logits, axis=1, keepdims=True)
    total = jnp.sum(terms, axis=0, keepdims=True)
    loss_in[me] = jnp.broadcast_to(total, (1, LANES))
    count = float(seeds * groups)
    gbuf[...] = (jnp.where(valid, jnp.exp(jnp.minimum(logits - lse, 0.0)), 0.0) - onehot) / count

    def loss_copy(p, slot):
        return remote(loss_in.at[slot], loss_in.at[slot], loss_ss.at[p], loss_rs.at[slot], p)

    acc[...] = jnp.zeros_like(acc)
    others(lambda p: loss_copy(p, me).start())

    def add_blocks(base, value):
        height = value.shape[0]
        for j in range(value.shape[1] // LANES):
            acc[base + j * height : base + (j + 1) * height, :] += value[:, j * LANES : (j + 1) * LANES]

    base2 = feat_dim * (hidden // LANES)
    base3 = base2 + hidden * (hidden // LANES)

    def backward(t, carry):
        at = pl.ds(pl.multiple_of(t * step_rows, step_rows), step_rows)
        x = rows[pl.ds(t * step_owners, step_owners)].reshape(step_rows, feat_dim)
        h1 = h1b[at, :]
        h2 = h2b[at, :]
        gz = (
            (wide(at).reshape(step_owners, seeds, padded) * gbuf[...][None])
            .reshape(step_rows, padded)
            .astype(BF16)
        )
        add_blocks(base3, tdot(h2, gz))
        d2 = jnp.where(h2 > 0, dott(gz, w3p[...]), 0.0).astype(BF16)
        add_blocks(base2, tdot(h1, d2))
        d1 = jnp.where(h1 > 0, dott(d2, w2[...]), 0.0).astype(BF16)
        add_blocks(0, tdot(x, d1))
        return carry

    lax.fori_loop(0, steps, backward, 0)

    half = chips * per

    def mine(c):
        return pl.ds(pl.multiple_of(core * half + c * per, 16), per)

    def theirs(c):
        return pl.ds(pl.multiple_of((1 - core) * half + c * per, 16), per)

    def chip_order(body):
        others(body, chips, chip)

    def pair_copy(c):
        return remote(pair_send.at[c], pair_recv.at[c], pair_ss.at[c], pair_rs.at[c], partner)

    def send_pair(c):
        pair_send[c] = acc[theirs(c), :].astype(BF16)
        pair_copy(c).start()

    chip_order(send_pair)
    send_pair(chip)

    def part_copy(c, slot):
        return remote(part_send.at[c], part_recv.at[slot], part_ss.at[c], part_rs.at[slot], c * 2 + core)

    def send_part(c):
        pair_copy(c).wait_recv()
        part_send[c] = (acc[mine(c), :] + pair_recv[c].astype(F32)).astype(BF16)
        part_copy(c, chip).start()

    chip_order(send_part)
    pair_copy(chip).wait_recv()
    stage_sum = acc[mine(chip), :] + pair_recv[chip].astype(F32)
    acc[mine(chip), :] = stage_sum

    def add_part(c):
        part_copy(c, c).wait_recv()
        acc[mine(chip), :] += part_recv[c].astype(F32)

    chip_order(add_part)
    full[core, chip] = acc[mine(chip), :].astype(BF16)

    def full_copy(c, slot):
        return remote(full.at[core, slot], full.at[core, slot], full_ss.at[c], full_rs.at[slot], c * 2 + core)

    def relay_copy(c, side):
        return remote(full.at[side, c], full.at[side, c], relay_ss.at[c], relay_rs.at[c], partner)

    chip_order(lambda c: full_copy(c, chip).start())
    relay_copy(chip, core).start()

    others(lambda p: loss_copy(p, p).wait_recv())
    loss_ref[...] = jnp.sum(loss_in[...], axis=0) / count

    def relay(c):
        full_copy(c, c).wait_recv()
        relay_copy(c, core).start()

    chip_order(relay)

    others(lambda p: row_copy(p, me).wait_send())
    others(lambda p: loss_copy(p, me).wait_send())

    def drain(c, carry):
        relay_copy(c, 1 - core).wait_recv()
        relay_copy(c, core).wait_send()
        pair_copy(c).wait_send()
        return carry

    lax.fori_loop(0, chips, drain, 0)
    chip_order(lambda c: part_copy(c, chip).wait_send())
    chip_order(lambda c: full_copy(c, chip).wait_send())

    flat = full[...].reshape(2 * half, LANES)

    def put(out, base, height, width):
        for j in range(-(-width // LANES)):
            cols = min(LANES, width - j * LANES)
            out[:, j * LANES : j * LANES + cols] = flat[base + j * height : base + (j + 1) * height, :cols]

    put(g1_ref, 0, feat_dim, hidden)
    put(g2_ref, base2, hidden, hidden)
    put(g3_ref, base3, hidden, classes)


def on_device(features, nbr_owner, nbr_local, ppr_weight, labels, w_first, w_second, w_third):
    groups = lax.axis_size("nodes")
    seeds, neighbours = nbr_owner.shape
    nodes, feat_dim = features.shape
    hidden, classes = w_third.shape
    padded = -(-classes // LANES) * LANES
    chips = groups // 2
    total = (feat_dim * hidden + hidden * hidden + hidden * padded) // LANES
    per = -(-total // (2 * chips * 16)) * 16
    pieces = 8
    table = jnp.arange(groups, dtype=jnp.int32)
    outgoing = jnp.sum(
        jnp.where(nbr_owner[None] == table[:, None, None], nbr_local[None], 0), axis=2
    )
    outgoing = jnp.pad(outgoing, ((0, 0), (0, LANES - seeds)))[:, None, :]
    dims = (groups, seeds, classes, per, pieces)
    vmem = pl.BlockSpec(memory_space=pltpu.VMEM)
    dma = pltpu.SemaphoreType.DMA
    loss, logits, g1, g2, g3 = pl.pallas_call(
        functools.partial(kernel, dims),
        out_shape=(
            jax.ShapeDtypeStruct((1, LANES), F32),
            jax.ShapeDtypeStruct((seeds, classes), F32),
            jax.ShapeDtypeStruct((feat_dim, hidden), BF16),
            jax.ShapeDtypeStruct((hidden, hidden), BF16),
            jax.ShapeDtypeStruct((hidden, classes), BF16),
        ),
        in_specs=[vmem] * 4 + [pl.BlockSpec(memory_space=pl.ANY)] + [vmem] * 3,
        out_specs=(vmem,) * 5,
        scratch_shapes=[
            pltpu.VMEM((nodes, feat_dim), BF16),
            pltpu.VMEM((nodes, feat_dim), F32),
            pltpu.VMEM((groups, 1, LANES), jnp.int32),
            pltpu.SMEM((groups, 1, LANES), jnp.int32),
            pltpu.VMEM((seeds, feat_dim), F32),
            pltpu.VMEM((groups, seeds, feat_dim), BF16),
            pltpu.VMEM((groups, seeds, feat_dim), BF16),
            pltpu.VMEM((groups * seeds, LANES), F32),
            pltpu.VMEM((hidden, padded), BF16),
            pltpu.VMEM((groups * seeds, hidden), BF16),
            pltpu.VMEM((groups * seeds, hidden), BF16),
            pltpu.VMEM((seeds, padded), F32),
            pltpu.VMEM((seeds, padded), F32),
            pltpu.VMEM((groups, 1, LANES), F32),
            pltpu.VMEM((2 * chips * per, LANES), F32),
            pltpu.VMEM((chips, per, LANES), BF16),
            pltpu.VMEM((chips, per, LANES), BF16),
            pltpu.VMEM((chips, per, LANES), BF16),
            pltpu.VMEM((chips, per, LANES), BF16),
            pltpu.VMEM((2, chips, per, LANES), BF16),
            dma((pieces,)),
            dma(()),
        ]
        + [dma((groups,))] * 6
        + [dma((chips,))] * 8,
        compiler_params=pltpu.CompilerParams(
            collective_id=0, has_side_effects=True, vmem_limit_bytes=60 * 1024 * 1024
        ),
        name="pprgo_step",
    )(outgoing, nbr_owner, ppr_weight, labels[:, None], features, w_first, w_second, w_third)
    return (loss[0, 0], logits, g1.astype(F32), g2.astype(F32), g3.astype(F32))


def solution(mesh):
    return jax.shard_map(
        on_device,
        mesh=mesh,
        in_specs=(
            P("nodes", None),
            P("nodes", None),
            P("nodes", None),
            P("nodes", None),
            P("nodes"),
            P(),
            P(),
            P(),
        ),
        out_specs=(P(), P("nodes", None), P(), P(), P()),
        check_vma=False,
    )
```

time: 219 us -> 68.2 us (0.31); the launches traced: 215 us -> 67.1 us
  waiting for transfers between devices: 100 us -> 0 us
  Pallas kernels: 0 us -> 52.7 us
  blocking collectives: 51.4 us -> 0 us
  local copies, waits for them, and re-layouts: 27.5 us -> 6.9 us
  between operations: 16 us -> 2.4 us
  matrix products: 10.9 us -> 0 us
  starting transfers between devices: 4.12 us -> 0 us
    psum x1 -> x0, waiting for transfers between devices: 91.7 us -> none  [on_device(): lax.psum((loss_terms, gradients[0], gradients[1], gradients[2]), 'nodes')]
    pallas_call x0 -> x1, Pallas kernels: none -> 52.7 us  [on_device(): pl.pallas_call(functools.partial(kernel, dims), out_shape=(jax.ShapeDtype...]
    psum x1 -> x0, blocking collectives: 39.7 us -> none  [on_device(): lax.psum((loss_terms, gradients[0], gradients[1], gradients[2]), 'nodes')]
    gather x5 -> x0, local copies, waits for them, and re-layouts: 16 us -> none  [the longest x3 7.2 us: on_device(): position = jnp.take_along_axis(earlier, nbr_owner, axis=1)]
    all_to_all x1 -> x0, blocking collectives: 11.7 us -> none  [on_device(): lax.all_to_all(outgoing.reshape(groups, capacity), 'nodes', split_axis=0,...]
    dot_general x7 -> x0, matrix products: 10.9 us -> none  [the longest x1 3.68 us: backward_rows(): jnp.dot(row_block.T, first_grad, preferred_element_type=jnp.float32)]
    all_to_all x1 -> x0, waiting for transfers between devices: 8.57 us -> none  [on_device(): lax.all_to_all(local_rows.reshape(groups, capacity, local_rows.shape[1]),...]
    scatter x1 -> x0, local copies, waits for them, and re-layouts: 4.31 us -> none  [on_device(): jnp.zeros((groups * capacity,), jnp.int32).at[slot_index]]
  transfers between devices with their start and end apart: 2 -> 0, of which waited for: 2 -> 0; matrix products, arithmetic and copies ran while one was open for 0% -> 0% of each run, Pallas kernels for 0% -> 0%
where the time goes in v1:
time: 68.2 us; the launch traced here: 67.1 us
  Pallas kernels  52.7 us (77%)
  local copies, waits for them, and re-layouts  6.9 us (10%)
  other arithmetic  5.12 us (8%)
  between operations  2.4 us (4%)
    pallas_call x1, Pallas kernels, on_device(): pl.pallas_call(functools.partial(kernel, dims), out_shape=(jax.ShapeDtype...  52.7 us
    unnamed x3, local copies, waits for them, and re-layouts  4.94 us
    convert_element_type x2, other arithmetic, on_device(): return (loss[0, 0], logits, g1.astype(F32), g2.astype(F32), g3.astype(F32))  3.78 us

profile of v1, /device:TPU:9, one launch (start us, length us, event | category | flops | bytes accessed | tf_op | source)
XLA Modules:
  0.0 67.1 jit_solution(11274731245413211478)
XLA Ops:
  0.6 1.8 %copy.17.w3 = bf16[512,172]{1,0:T(8,128)(2,1)} copy(bf16[512,172]{0,1:T(8,128)(2,1)} %param.15) | data formatting | bytes 352256 | tf_op args[7]
  2.4 1.3 %select_reduce_fusion = s32[32,32]{1,0:T(8,128)S(1)} fusion(s32[32,32]{1,0:T(8,128)} %param.10, s32[32,32]{1,0:T(8,128)} %owner.1), kind=kLoop, calls=%fused_computation | loop fusion | flops 97280 | bytes 12288 | tf_op jit(solution)/shard_map/reduce_sum | solution.py:281
  3.7 0.6 pad.4
  4.4 1.3 %copy.16.labels = s32[32,1]{1,0:T(8,128)} copy(s32[32,1]{0,1:T(1,128)} %bitcast.5) | data formatting | bytes 256 | tf_op jit(solution)/shard_map/broadcast_in_dim | solution.py:329
  5.7 52.7 %pprgo_step.1 = (f32[1,128]{1,0:T(1,128)}, f32[32,172]{1,0:T(8,128)}, bf16[128,512]{1,0:T(8,128)(2,1)}, bf16[512,512]{1,0:T(8,128)(2,1)}, bf16[512,172]{1,0:T(8,128)(2,1)}) custom-call(s32[32,1,128]{2,1,0:T(1,128)} %bitcast.4, s32[32,32]{1,0:T(8,128)} %owner.1, f32[32,32]{1,0:T(8,128)} %ppr.1, s32[32,1]{1,0:T(8,128)} %copy.16.labels, ...), custom_call_target="tpu_custom_call" | custom-call | tf_op jit(solution)/shard_map/pprgo_step/pallas_call | solution.py:288
  58.4 2.1 %convert_element_type.10 = f32[512,512]{1,0:T(8,128)} convert(bf16[512,512]{1,0:T(8,128)(2,1)} %get-tuple-element.13) | non-fusion elementwise | flops 262144 | bytes 1572864 | tf_op jit(solution)/shard_map/convert_element_type | solution.py:330
  60.6 1.8 %copy.18 = f32[512,172]{0,1:T(8,128)} copy(bf16[512,172]{1,0:T(8,128)(2,1)} %get-tuple-element.14) | data formatting | bytes 528384
  62.4 1.6 %convert_element_type.9 = f32[128,512]{1,0:T(8,128)} convert(bf16[128,512]{1,0:T(8,128)(2,1)} %get-tuple-element.12) | non-fusion elementwise | flops 65536 | bytes 393216 | tf_op jit(solution)/shard_map/convert_element_type | solution.py:330
  64.6 1.4 %copy.22 = f32[32,172]{1,0:T(8,128)} copy(f32[32,172]{1,0:T(8,128)} %get-tuple-element.31) | data formatting | bytes 44032

commit v2 on v1

--- a/solution.py
+++ b/solution.py
@@ -23,9 +23,9 @@
 
 def kernel(
     dims,
-    idx_out, owner, ppr, labels, feats, w1, w2, w3,
-    loss_ref, logits_ref, g1_ref, g2_ref, g3_ref,
-    feat16, feat32, idx_in, idx_smem, stage, row_send, rows, wbuf, w3p, h1b, h2b,
+    owner, local, ppr, labels, feats, w1, w2, w3t,
+    loss_ref, logits_ref, flat_ref,
+    square, idx_out, feat16, feat32, idx_in, idx_smem, stage, row_send, rows, wbuf, w3p, h1b, h2b,
     zacc, gbuf, loss_in, acc, pair_send, pair_recv, part_send, part_recv, full,
     feat_sem, smem_sem, idx_ss, idx_rs, row_ss, row_rs, loss_ss, loss_rs,
     pair_ss, pair_rs, part_ss, part_rs, full_ss, full_rs, relay_ss, relay_rs,
@@ -38,7 +38,8 @@
     partner = chip * 2 + (1 - core)
     nodes, feat_dim = feats.shape
     hidden = w1.shape[1]
-    padded = w3p.shape[1]
+    padded = w3p.shape[0]
+    class_rows = -(-classes // 16) * 16
     piece = nodes // pieces
 
     def remote(src, dst, ss, rs, dev):
@@ -61,6 +62,24 @@
 
     barrier = pltpu.get_barrier_semaphore()
     others(lambda p: pl.semaphore_signal(barrier, inc=1, device_id=(p,), device_id_type=MESH))
+
+    own = owner[...]
+    neighbours = own.shape[1]
+
+    def turned(value, fill):
+        square[...] = jnp.full_like(square, fill)
+        square[:seeds, :neighbours] = value
+        return jnp.transpose(square[...])[:neighbours, :]
+
+    own_t = turned(own, -1)
+    local_t = turned(local[...], 0)
+
+    def index_step(o, carry):
+        hit = jnp.where(own_t == o, local_t, 0)
+        idx_out[o] = jnp.sum(hit, axis=0, keepdims=True)
+        return carry
+
+    lax.fori_loop(0, groups, index_step, 0)
     pl.semaphore_wait(barrier, groups - 1)
 
     def idx_copy(p, slot):
@@ -70,9 +89,8 @@
     idx_in[me] = idx_out[me]
 
     w3p[...] = jnp.zeros_like(w3p)
-    w3p[:, :classes] = w3[...]
-
-    own = owner[...]
+    w3p[:classes, :] = w3t[...]
+
     score = ppr[...]
 
     def weight_step(o, carry):
@@ -130,7 +148,7 @@
         h1b[at, :] = h1
         h2 = jnp.maximum(jnp.dot(h1, w2[...], preferred_element_type=F32), 0.0).astype(BF16)
         h2b[at, :] = h2
-        z = jnp.dot(h2, w3p[...], preferred_element_type=F32) * wide(at)
+        z = dott(h2, w3p[...]) * wide(at)
         zacc[...] += jnp.sum(z.reshape(step_owners, seeds, padded), axis=0)
         return carry
 
@@ -143,7 +161,11 @@
     highest = jnp.max(jnp.where(valid, logits, -3.0e38), axis=1, keepdims=True)
     expd = jnp.where(valid, jnp.exp(jnp.minimum(logits - highest, 0.0)), 0.0)
     lse = jnp.log(jnp.sum(expd, axis=1, keepdims=True)) + highest
-    onehot = jnp.where(col == labels[...], 1.0, 0.0)
+    eye = lax.broadcasted_iota(jnp.int32, (seeds, seeds), 0) == lax.broadcasted_iota(
+        jnp.int32, (seeds, seeds), 1
+    )
+    label = jnp.sum(jnp.where(eye, labels[...].astype(F32), 0.0), axis=1, keepdims=True)
+    onehot = jnp.where(col.astype(F32) == label, 1.0, 0.0)
     terms = lse - jnp.sum(onehot * logits, axis=1, keepdims=True)
     total = jnp.sum(terms, axis=0, keepdims=True)
     loss_in[me] = jnp.broadcast_to(total, (1, LANES))
@@ -174,8 +196,8 @@
             .reshape(step_rows, padded)
             .astype(BF16)
         )
-        add_blocks(base3, tdot(h2, gz))
-        d2 = jnp.where(h2 > 0, dott(gz, w3p[...]), 0.0).astype(BF16)
+        add_blocks(base3, tdot(gz, h2)[:class_rows])
+        d2 = jnp.where(h2 > 0, jnp.dot(gz, w3p[...], preferred_element_type=F32), 0.0).astype(BF16)
         add_blocks(base2, tdot(h1, d2))
         d1 = jnp.where(h1 > 0, dott(d2, w2[...]), 0.0).astype(BF16)
         add_blocks(0, tdot(x, d1))
@@ -186,10 +208,10 @@
     half = chips * per
 
     def mine(c):
-        return pl.ds(pl.multiple_of(core * half + c * per, 16), per)
+        return pl.ds(pl.multiple_of(core * half + c * per, 8), per)
 
     def theirs(c):
-        return pl.ds(pl.multiple_of((1 - core) * half + c * per, 16), per)
+        return pl.ds(pl.multiple_of((1 - core) * half + c * per, 8), per)
 
     def chip_order(body):
         others(body, chips, chip)
@@ -255,16 +277,19 @@
     chip_order(lambda c: part_copy(c, chip).wait_send())
     chip_order(lambda c: full_copy(c, chip).wait_send())
 
-    flat = full[...].reshape(2 * half, LANES)
-
-    def put(out, base, height, width):
-        for j in range(-(-width // LANES)):
-            cols = min(LANES, width - j * LANES)
-            out[:, j * LANES : j * LANES + cols] = flat[base + j * height : base + (j + 1) * height, :cols]
-
-    put(g1_ref, 0, feat_dim, hidden)
-    put(g2_ref, base2, hidden, hidden)
-    put(g3_ref, base3, hidden, classes)
+    flat_ref[...] = full[...].reshape(2 * half, LANES)
+
+
+def widen_kernel(loss, logits, flat, loss_ref, logits_ref, g1_ref, g2_ref, g3_ref):
+    loss_ref[...] = loss[:, :1]
+    logits_ref[...] = logits[...]
+    base = 0
+    for out in (g1_ref, g2_ref, g3_ref):
+        height, width = out.shape
+        stride = -(-height // 16) * 16
+        for j in range(width // LANES):
+            out[:, j * LANES : (j + 1) * LANES] = flat[base : base + height, :].astype(F32)
+            base += stride
 
 
 def on_device(features, nbr_owner, nbr_local, ppr_weight, labels, w_first, w_second, w_third):
@@ -274,29 +299,25 @@
     hidden, classes = w_third.shape
     padded = -(-classes // LANES) * LANES
     chips = groups // 2
-    total = (feat_dim * hidden + hidden * hidden + hidden * padded) // LANES
-    per = -(-total // (2 * chips * 16)) * 16
+    class_rows = -(-classes // 16) * 16
+    total = (feat_dim + hidden + class_rows) * (hidden // LANES)
+    per = -(-total // (2 * chips * 8)) * 8
     pieces = 8
-    table = jnp.arange(groups, dtype=jnp.int32)
-    outgoing = jnp.sum(
-        jnp.where(nbr_owner[None] == table[:, None, None], nbr_local[None], 0), axis=2
-    )
-    outgoing = jnp.pad(outgoing, ((0, 0), (0, LANES - seeds)))[:, None, :]
     dims = (groups, seeds, classes, per, pieces)
     vmem = pl.BlockSpec(memory_space=pltpu.VMEM)
     dma = pltpu.SemaphoreType.DMA
-    loss, logits, g1, g2, g3 = pl.pallas_call(
+    loss, logits, flat = pl.pallas_call(
         functools.partial(kernel, dims),
         out_shape=(
             jax.ShapeDtypeStruct((1, LANES), F32),
             jax.ShapeDtypeStruct((seeds, classes), F32),
-            jax.ShapeDtypeStruct((feat_dim, hidden), BF16),
-            jax.ShapeDtypeStruct((hidden, hidden), BF16),
-            jax.ShapeDtypeStruct((hidden, classes), BF16),
+            jax.ShapeDtypeStruct((2 * chips * per, LANES), BF16),
         ),
         in_specs=[vmem] * 4 + [pl.BlockSpec(memory_space=pl.ANY)] + [vmem] * 3,
-        out_specs=(vmem,) * 5,
+        out_specs=(vmem,) * 3,
         scratch_shapes=[
+            pltpu.VMEM((LANES, LANES), jnp.int32),
+            pltpu.VMEM((groups, 1, LANES), jnp.int32),
             pltpu.VMEM((nodes, feat_dim), BF16),
             pltpu.VMEM((nodes, feat_dim), F32),
             pltpu.VMEM((groups, 1, LANES), jnp.int32),
@@ -305,7 +326,7 @@
             pltpu.VMEM((groups, seeds, feat_dim), BF16),
             pltpu.VMEM((groups, seeds, feat_dim), BF16),
             pltpu.VMEM((groups * seeds, LANES), F32),
-            pltpu.VMEM((hidden, padded), BF16),
+            pltpu.VMEM((padded, hidden), BF16),
             pltpu.VMEM((groups * seeds, hidden), BF16),
             pltpu.VMEM((groups * seeds, hidden), BF16),
             pltpu.VMEM((seeds, padded), F32),
@@ -326,8 +347,24 @@
             collective_id=0, has_side_effects=True, vmem_limit_bytes=60 * 1024 * 1024
         ),
         name="pprgo_step",
-    )(outgoing, nbr_owner, ppr_weight, labels[:, None], features, w_first, w_second, w_third)
-    return (loss[0, 0], logits, g1.astype(F32), g2.astype(F32), g3.astype(F32))
+    )(
+        nbr_owner, nbr_local, ppr_weight, labels.reshape(1, seeds), features,
+        w_first, w_second, w_third.T,
+    )
+    loss, logits, g1, g2, g3 = pl.pallas_call(
+        widen_kernel,
+        out_shape=(
+            jax.ShapeDtypeStruct((1, 1), F32),
+            jax.ShapeDtypeStruct((seeds, classes), F32),
+            jax.ShapeDtypeStruct((feat_dim, hidden), F32),
+            jax.ShapeDtypeStruct((hidden, hidden), F32),
+            jax.ShapeDtypeStruct((classes, hidden), F32),
+        ),
+        in_specs=[vmem] * 3,
+        out_specs=(vmem,) * 5,
+        name="widen",
+    )(loss, logits, flat)
+    return (loss.reshape(()), logits, g1, g2, g3.T)
 
 
 def solution(mesh):

time: 68.2 us -> 55 us (0.81); the launches traced: 67.1 us -> 54.8 us
  local copies, waits for them, and re-layouts: 6.9 us -> 0 us
  other arithmetic: 5.12 us -> 0 us
  between operations: 2.4 us -> 0.64 us
  Pallas kernels: 52.7 us -> 54.2 us
    unnamed x3 -> x0, local copies, waits for them, and re-layouts: 4.94 us -> none
    convert_element_type x2 -> x0, other arithmetic: 3.78 us -> none  [on_device(): return (loss[0, 0], logits, g1.astype(F32), g2.astype(F32), g3.astype(F32))]
    pallas_call x0 -> x1, Pallas kernels: none -> 2.49 us  [on_device(): pl.pallas_call(widen_kernel, out_shape=(jax.ShapeDtypeStruct((1, 1), F32)...]
    reduce_sum x1 -> x0, other arithmetic: 1.35 us -> none  [on_device(): jnp.sum(jnp.where(nbr_owner[None] == table[:, None, None], nbr_local[None...]
    broadcast_in_dim x1 -> x0, local copies, waits for them, and re-layouts: 1.34 us -> none  [on_device(): labels[:, None]]
    pallas_call x1, Pallas kernels: 52.7 us -> 51.7 us  [on_device(): pl.pallas_call(functools.partial(kernel, dims), out_shape=(jax.ShapeDtype...]
where the time goes in v2:
time: 55 us; the launch traced here: 54.8 us
  Pallas kernels  54.2 us (99%)
  between operations  0.64 us (1%)
    pallas_call x1, Pallas kernels, on_device(): pl.pallas_call(functools.partial(kernel, dims), out_shape=(jax.ShapeDtype...  51.7 us
    pallas_call x1, Pallas kernels, on_device(): pl.pallas_call(widen_kernel, out_shape=(jax.ShapeDtypeStruct((1, 1), F32)...  2.49 us

profile of v2, /device:TPU:9, one launch (start us, length us, event | category | flops | bytes accessed | tf_op | source)
XLA Modules:
  0.0 54.8 jit_solution(3579765050795880791)
XLA Ops:
  0.6 51.7 %pprgo_step.1 = (f32[1,128]{1,0:T(1,128)}, f32[32,172]{1,0:T(8,128)}, bf16[3328,128]{1,0:T(8,128)(2,1)}) custom-call(s32[32,32]{1,0:T(8,128)} %owner.1, s32[32,32]{1,0:T(8,128)} %local.1, f32[32,32]{1,0:T(8,128)} %ppr.1, s32[1,32]{1,0:T(1,128)} %bitcast.5, bf16[16384,128]{1,0:T(8,128)(2,1)} %feats.1, bf16[128,512]{1,0:T(8,128)(2,1)} %w1.1, ...), custom_call_target="tpu_custom_call" | custom-call | tf_op jit(solution)/shard_map/pprgo_step/pallas_call | solution.py:309
  52.3 2.5 %widen.1 = (f32[1,1]{1,0:T(1,128)}, f32[32,172]{1,0:T(8,128)}, f32[128,512]{1,0:T(8,128)}, f32[512,512]{1,0:T(8,128)}, f32[172,512]{1,0:T(8,128)}) custom-call(f32[1,128]{1,0:T(1,128)} %get-tuple-element.13.loss, f32[32,172]{1,0:T(8,128)} %get-tuple-element.14.logits, bf16[3328,128]{1,0:T(8,128)(2,1)} %get-tuple-element.15.flat), custom_call_target="tpu_custom_call" | custom-call | tf_op jit(solution)/shard_map/widen/pallas_call | solution.py:354
